TPU v7x, 32 devices: a whole 2x2x4 slice. The times are simulated.
32 devices in a mesh: img: 4 (over x, core), rows: 8 (over z, y).
Axes of the slice: x: 2, y: 2, z: 4, core: 2. Of those that a mesh axis runs over, the one named last changes fastest.
Arguments:
- feat_fine: bfloat16 [256, 128, 256], P(('img', 'rows')), parts along dimension 0, may hold values from -6 to 6
- feat_second: bfloat16 [128, 64, 256], P(('img', 'rows')), parts along dimension 0, may hold values from -6 to 6
- feat_third: bfloat16 [64, 32, 256], P(('img', 'rows')), parts along dimension 0, may hold values from -6 to 6
- conv_weight: bfloat16 [10, 9, 256, 256], replicated, may hold values from -0.125 to 0.125
- conv_bias: float32 [10, 256], replicated, may hold values from -3 to 3
- out_weight: bfloat16 [3, 256, 256], replicated, may hold values from -0.375 to 0.375
- out_bias: float32 [3, 256], replicated, may hold values from -3 to 3
Outputs:
- joined: bfloat16 [512, 256, 256], P(('img', 'rows')), parts along dimension 0
There are 4 independent parts, one for each index of `img`. A program takes and returns all parts, laid end to end along the dimension named above; an argument that names none is the same for every part. Nothing has to cross between parts.
All inputs are finite; a program needn't handle non-finite values.
Results may differ from a plain program's by a relative error of at most 0.015.
Values may be sent and summed in bfloat16 or wider, within the bound.
A program may use at most 128 MiB of HBM per device.

v0:
```python
import functools

import jax
import jax.numpy as jnp
from jax import lax
from jax.experimental import pallas as pl
from jax.experimental.pallas import tpu as pltpu
from jax.sharding import PartitionSpec as P

MESH = pl.DeviceIdType.MESH
LANES = 16
FINE, SECOND, THIRD = 0, 1, 2
HALOS = (5, 6, 5)
WEIGHT_ORDER = (6, 0, 1, 2, 3, 4, 5, 7, 8, 9)


def direct_sends(blocks):
    plan = []
    for level in (THIRD, SECOND, FINE):
        block, halo = blocks[level], HALOS[level]
        for distance in range(1, -(-halo // block) + 1):
            if level == THIRD or distance > 1:
                plan.append((level, distance, min(block, halo - (distance - 1) * block)))
    return plan


def pair_chunks(level, block):
    near = min(block, HALOS[level])
    lead = near - near // 2 if level == FINE else near
    cuts = ((0, lead), (lead, near), (near, block))
    return [(a, block - b, b - a, b <= near) for a, b in cuts if b > a]


def edge_steps(values, clamp):
    steps = values.shape[1]
    first, last = values[:, 0], values[:, steps - 1]
    place = lax.broadcasted_iota(jnp.int32, first.shape, 1)
    zero = jnp.zeros_like(first)
    before = jnp.where(place == 0, first if clamp else zero, pltpu.roll(last, 1, 1))
    after = jnp.where(place == LANES - 1, last if clamp else zero, pltpu.roll(first, LANES - 1, 1))
    return before, after


def kernel(
    devices, fine_ref, second_ref, third_ref, conv_hbm, bias_ref, proj_hbm, proj_bias_ref, refined_f,
    fine_up, fine_down, second_up, second_down, third_up, third_down,
    fine_peer, fine_far, second_peer, second_far, fine_x, second_x, third_x, stage,
    weights, projs, padded_f, hidden_f, merged_f, path_f, padded_s, hidden_s, merged_s, path_s,
    padded_t, hidden_t, refined_s, refined_t, proj_y,
    up_send, up_recv, down_send, down_recv,
    pair_send, pair_recv, far_send, far_recv, weight_sem, proj_sem,
):
    me = lax.axis_index("rows")
    own = (fine_ref, second_ref, third_ref)
    ups = (fine_up, second_up, third_up)
    downs = (fine_down, second_down, third_down)
    blocks = tuple(ref.shape[0] for ref in own)
    plan = direct_sends(blocks)
    fields = (fine_x, second_x, third_x)
    peers = (fine_peer, second_peer)
    fars = (fine_far, second_far)
    odd = me % 2
    even = odd == 0
    partner = me + 1 - 2 * odd
    target = me + 2 - 4 * odd
    source = me - 2 + 4 * odd
    reach = max(distance for _, distance, _ in plan)

    weight_copies = {
        k: pltpu.make_async_copy(conv_hbm.at[k], weights.at[k], weight_sem.at[k])
        for k in WEIGHT_ORDER
    }
    proj_copy = pltpu.make_async_copy(proj_hbm, projs, proj_sem)
    for at, k in enumerate(WEIGHT_ORDER):
        weight_copies[k].start()
        if at == 2:
            proj_copy.start()

    barrier = pltpu.get_barrier_semaphore()
    for distance in range(1, reach + 1):
        @pl.when(me >= distance)
        def _():
            pl.semaphore_signal(barrier, inc=1, device_id={"rows": me - distance}, device_id_type=MESH)

        @pl.when(me + distance < devices)
        def _():
            pl.semaphore_signal(barrier, inc=1, device_id={"rows": me + distance}, device_id_type=MESH)
    expected = jnp.minimum(me, reach) + jnp.minimum(devices - 1 - me, reach)
    pl.semaphore_wait(barrier, expected)

    up_copies, down_copies = [], []
    for at, (level, distance, rows) in enumerate(plan):
        block, halo = blocks[level], HALOS[level]
        up_at = halo - (distance - 1) * block - rows
        down_at = (distance - 1) * block
        up_copies.append(pltpu.make_async_remote_copy(
            src_ref=own[level].at[pl.ds(block - rows, rows)],
            dst_ref=ups[level].at[pl.ds(up_at, rows)],
            send_sem=up_send.at[at], recv_sem=up_recv.at[at],
            device_id={"rows": me + distance}, device_id_type=MESH))
        down_copies.append(pltpu.make_async_remote_copy(
            src_ref=own[level].at[pl.ds(0, rows)],
            dst_ref=downs[level].at[pl.ds(down_at, rows)],
            send_sem=down_send.at[at], recv_sem=down_recv.at[at],
            device_id={"rows": me - distance}, device_id_type=MESH))
        if level == THIRD:
            pl.when(me + distance < devices)(up_copies[at].start)
            pl.when(me >= distance)(down_copies[at].start)

    pair_copies, far_copies = {FINE: [], SECOND: []}, {FINE: [], SECOND: []}
    serial = 0
    for level in (SECOND, FINE):
        block = blocks[level]
        near = min(block, HALOS[level])
        for even_at, odd_at, rows, forwarded in pair_chunks(level, block):
            at = even_at + odd * (odd_at - even_at)
            pair_copies[level].append(pltpu.make_async_remote_copy(
                src_ref=own[level].at[pl.ds(at, rows)], dst_ref=peers[level].at[pl.ds(at, rows)],
                send_sem=pair_send.at[serial], recv_sem=pair_recv.at[serial],
                device_id={"rows": partner}, device_id_type=MESH))
            if forwarded:
                held = odd_at + odd * (even_at - odd_at)
                spot = held - (1 - odd) * (block - near)
                far_copies[level].append(pltpu.make_async_remote_copy(
                    src_ref=peers[level].at[pl.ds(held, rows)], dst_ref=fars[level].at[pl.ds(spot, rows)],
                    send_sem=far_send.at[serial], recv_sem=far_recv.at[serial],
                    device_id={"rows": target}, device_id_type=MESH))
            serial += 1
            pair_copies[level][-1].start()
        for at, (wanted, distance, _) in enumerate(plan):
            if wanted == level:
                pl.when(me + distance < devices)(up_copies[at].start)
                pl.when(me >= distance)(down_copies[at].start)
    has_target = jnp.logical_and(target >= 0, target < devices)
    has_source = jnp.logical_and(source >= 0, source < devices)

    def pass_on(level, chunk):
        pair_copies[level][chunk].wait_recv()
        if chunk < len(far_copies[level]):
            pl.when(has_target)(far_copies[level][chunk].start)

    def arrive(wanted):
        for at, (level, distance, _) in enumerate(plan):
            if level == wanted:
                pl.when(me >= distance)(up_copies[at].wait_recv)
                pl.when(me + distance < devices)(down_copies[at].wait_recv)
        for copy in far_copies.get(wanted, ()):
            pl.when(has_source)(copy.wait_recv)

    def inside(level, row):
        block = blocks[level]
        if 0 <= row < block:
            return None
        place = me * block + row
        return jnp.logical_and(place >= 0, place < devices * block)

    def store_padded(ref, at, values, level, first_row):
        steps = values.shape[1]
        for r in range(values.shape[0]):
            row = values[r:r + 1].astype(jnp.float32)
            valid = inside(level, first_row + r)
            if valid is not None:
                row = jnp.where(valid, row, 0.0)
            before, after = edge_steps(row, False)
            ref[at + r, 1:steps + 1] = row[0].astype(jnp.bfloat16)
            ref[at + r, 0] = before[0].astype(jnp.bfloat16)
            ref[at + r, steps + 1] = after[0].astype(jnp.bfloat16)

    def conv(ref, k, first, last, emit):
        steps = ref.shape[1] - 2
        tile = max(1, 512 // (steps * LANES))
        for r in range(first, last, tile):
            rows = min(tile, last - r)
            flat = jnp.concatenate(
                [ref[r + a:r + a + rows, b:b + steps].reshape(rows * steps * LANES, -1)
                 for a in range(3) for b in range(3)], axis=1)
            acc = jnp.dot(flat, weights[k], preferred_element_type=jnp.float32)
            acc = acc + bias_ref[k:k + 1, :]
            emit(r, acc.reshape(rows, steps, LANES, -1))

    def raw_row(level, place):
        block, halo = blocks[level], HALOS[level]
        near = min(block, halo)
        if 0 <= place < block:
            return own[level][place]
        if place < 0:
            j = -1 - place
            row = ups[level][halo - 1 - j] if level == THIRD or j >= block else None
            if row is None:
                row = jnp.where(even, fars[level][near - 1 - j], peers[level][block - 1 - j])
            return row
        j = place - block
        if level == THIRD or j >= block:
            return downs[level][j]
        return jnp.where(even, peers[level][j], fars[level][j])

    def take_rows(level, padded, first, last):
        halo = HALOS[level]
        columns = own[level].shape[1]
        steps = columns // LANES
        width = stage.shape[3]
        for place in range(first, last):
            row = raw_row(level, place).astype(jnp.float32)
            slot = place % stage.shape[0]
            parts = range(row.shape[1] // width)
            for c in parts:
                stage[slot, c, 0:columns] = row[:, c * width:(c + 1) * width]
            turned = jnp.concatenate(
                [jnp.concatenate([stage[slot, c, pl.ds(t, LANES, stride=steps), :] for c in parts], axis=1)[None]
                 for t in range(steps)], axis=0)
            fields[level][halo + place] = turned.astype(jnp.bfloat16)
            store_padded(padded, halo + place, jnp.maximum(turned, 0.0)[None], level, place)

    def hidden(level, source, target, k, first, last, row0):
        def emit(r, acc):
            store_padded(target, r, jnp.maximum(acc, 0.0), level, row0 + r)
        conv(source, k, first, last, emit)

    def source_rows(level, row, rows):
        at = HALOS[level] + row
        return fields[level][at:at + rows].astype(jnp.float32)

    def lift(level, refined, halo, index, emit, extra):
        count, steps = refined.shape[0], refined.shape[1]
        block = blocks[level]
        w = projs[index]
        tile = max(1, 512 // (steps * LANES))
        for r in range(0, count, tile):
            rows = min(tile, count - r)
            y = jnp.dot(refined[r:r + rows].reshape(rows * steps * LANES, -1), w,
                        preferred_element_type=jnp.float32)
            proj_y[r:r + rows, 0:steps] = y.reshape(rows, steps, LANES, -1)

        def line(m):
            value = proj_y[m, 0:steps]
            before, after = halo - 1 - m, m - halo - block
            if before >= 0 and before % block == 0:
                value = jnp.where(me == before // block, proj_y[m + 1, 0:steps], value)
            if after >= 0 and after % block == 0:
                value = jnp.where(me == devices - 1 - after // block, proj_y[m - 1, 0:steps], value)
            return value

        bias = proj_bias_ref[index:index + 1, :]

        def columns(out_row, major, minor):
            row = (0.75 * major + 0.25 * minor + bias)[None]
            before, after = edge_steps(row, True)
            wide = jnp.concatenate([before[:, None], row, after[:, None]], axis=1)[0]
            low = 0.25 * wide[0:steps] + 0.75 * row[0]
            high = 0.75 * row[0] + 0.25 * wide[2:steps + 2]
            emit(out_row, low.astype(jnp.bfloat16), high.astype(jnp.bfloat16))

        for m in range(count):
            even = 2 * (m - halo)
            if 1 <= m and (m < count - 1 or extra):
                columns(even, line(m), line(m - 1))
            if m < count - 1 and (m >= 1 or extra):
                columns(even + 1, line(m), line(m + 1))

    def emit_to(ref, first):
        def emit(row, low, high):
            for t in range(low.shape[0]):
                ref[row - first, 2 * t] = low[t]
                ref[row - first, 2 * t + 1] = high[t]
        return emit

    halo_f, halo_s, halo_t = HALOS
    block_f, block_s, block_t = blocks
    take_rows(FINE, padded_f, 0, block_f)
    weight_copies[6].wait()
    hidden(FINE, padded_f, hidden_f, 6, halo_f, halo_f + block_f - 2, 1 - halo_f)

    take_rows(THIRD, padded_t, 0, block_t)
    take_rows(SECOND, padded_s, 0, block_s)
    arrive(THIRD)
    take_rows(THIRD, padded_t, -halo_t, 0)
    take_rows(THIRD, padded_t, block_t, block_t + halo_t)
    pass_on(SECOND, 0)
    weight_copies[0].wait()
    hidden(THIRD, padded_t, hidden_t, 0, 0, block_t + 2 * halo_t - 2, 1 - halo_t)
    weight_copies[1].wait()

    def emit_third(r, acc):
        rows = acc.shape[0]
        total = acc + source_rows(THIRD, r + 2 - halo_t, rows)
        refined_t[r:r + rows] = total.astype(jnp.bfloat16)

    conv(hidden_t, 1, 0, block_t + 2 * halo_t - 4, emit_third)
    proj_copy.wait()
    lift(THIRD, refined_t, halo_t - 2, 0, emit_to(path_s, 2 - halo_s), False)

    def join(level, halo, padded, hidden_ref, merged, path, refined, k, early):
        block = blocks[level]
        last = block + 2 * halo
        if early:
            hidden(level, padded, hidden_ref, k, 0, early[0], 1 - halo)
            hidden(level, padded, hidden_ref, k, early[1], last - 2, 1 - halo)
        else:
            weight_copies[k].wait()
            hidden(level, padded, hidden_ref, k, 0, last - 2, 1 - halo)
        weight_copies[k + 1].wait()

        def emit_merged(r, acc):
            rows = acc.shape[0]
            total = acc + source_rows(level, r + 2 - halo, rows) + path[r:r + rows].astype(jnp.float32)
            total = total.astype(jnp.bfloat16)
            merged[r:r + rows] = total
            store_padded(padded, r, jnp.maximum(total, 0), level, r + 2 - halo)

        conv(hidden_ref, k + 1, 0, last - 4, emit_merged)
        if level == SECOND:
            pass_on(FINE, 1)
        weight_copies[k + 2].wait()
        hidden(level, padded, hidden_ref, k + 2, 0, last - 6, 3 - halo)
        weight_copies[k + 3].wait()

        def emit_refined(r, acc):
            rows = acc.shape[0]
            total = acc + merged[r + 2:r + 2 + rows].astype(jnp.float32)
            refined[r:r + rows] = total.astype(jnp.bfloat16)

        conv(hidden_ref, k + 3, 0, last - 8, emit_refined)

    pass_on(FINE, 0)
    arrive(SECOND)
    take_rows(SECOND, padded_s, -halo_s, 0)
    take_rows(SECOND, padded_s, block_s, block_s + halo_s)
    join(SECOND, halo_s, padded_s, hidden_s, merged_s, path_s, refined_s, 2, None)
    lift(SECOND, refined_s, halo_s - 4, 1, emit_to(path_f, 2 - halo_f), True)

    pass_on(FINE, 2)
    arrive(FINE)
    take_rows(FINE, padded_f, -halo_f, 0)
    take_rows(FINE, padded_f, block_f, block_f + halo_f)
    join(FINE, halo_f, padded_f, hidden_f, merged_f, path_f, refined_f, 6,
         (halo_f, halo_f + block_f - 2))

    for at, (_, distance, _) in enumerate(plan):
        pl.when(me + distance < devices)(up_copies[at].wait_send)
        pl.when(me >= distance)(down_copies[at].wait_send)
    for level in (SECOND, FINE):
        for copy in pair_copies[level]:
            copy.wait_send()
        for copy in far_copies[level]:
            pl.when(has_target)(copy.wait_send)


def lift_kernel(devices, index, refined_ref, proj_ref, bias_ref, out_ref, lines, stage):
    me = lax.axis_index("rows")
    at = pl.program_id(0)
    count, steps = refined_ref.shape[0], refined_ref.shape[1]
    per = out_ref.shape[0] // 2
    channels = refined_ref.shape[3]
    width = stage.shape[3]

    @pl.when(at == 0)
    def _():
        for m in range(0, count, 2):
            rows = min(2, count - m)
            y = jnp.dot(refined_ref[m:m + rows].reshape(rows * steps * LANES, channels), proj_ref[0],
                        preferred_element_type=jnp.float32)
            lines[m:m + rows] = y.reshape(rows, steps, LANES, channels)
        lines[0] = jnp.where(me == 0, lines[1], lines[0])
        lines[count - 1] = jnp.where(me == devices - 1, lines[count - 2], lines[count - 1])

    bias = bias_ref[index:index + 1, :]
    for i in range(per):
        m = 1 + at * per + i
        for half in range(2):
            row = 0.75 * lines[m] + 0.25 * lines[m - 1 + 2 * half] + bias
            before, after = edge_steps(row[None], True)
            for t in range(steps):
                low = 0.25 * (row[t - 1] if t else before[0]) + 0.75 * row[t]
                high = 0.75 * row[t] + 0.25 * (row[t + 1] if t < steps - 1 else after[0])
                for c in range(channels // width):
                    part = slice(c * width, (c + 1) * width)
                    stage[2 * i + half, c, pl.ds(2 * t, LANES, stride=2 * steps), :] = low[:, part]
                    stage[2 * i + half, c, pl.ds(2 * t + 1, LANES, stride=2 * steps), :] = high[:, part]
            for c in range(channels // width):
                out_ref[2 * i + half, :, c * width:(c + 1) * width] = stage[2 * i + half, c].astype(jnp.bfloat16)


def local(devices, feat_fine, feat_second, feat_third, conv_weight, conv_bias, out_weight, out_bias):
    fields = (feat_fine, feat_second, feat_third)
    channels = feat_fine.shape[2]
    blocks = [v.shape[0] for v in fields]
    columns = [v.shape[1] for v in fields]
    steps = [c // LANES for c in columns]
    width = min(128, channels)

    def raw(count, level):
        return pltpu.VMEM((count, columns[level], channels), jnp.bfloat16)

    def rows_of(count, level, extra=0, dtype=jnp.bfloat16):
        return pltpu.VMEM((count, steps[level] + extra, LANES, channels), dtype)

    extents = [block + 2 * halo for block, halo in zip(blocks, HALOS)]
    copies = len(direct_sends(blocks))
    pairs = sum(len(pair_chunks(level, blocks[level])) for level in (FINE, SECOND))
    dma = pltpu.SemaphoreType.DMA
    scratch = [raw(HALOS[level], level) for level in range(3) for _ in range(2)]
    for level in (FINE, SECOND):
        scratch += [raw(blocks[level], level), raw(min(blocks[level], HALOS[level]), level)]
    scratch += [rows_of(extents[level], level) for level in range(3)]
    scratch += [pltpu.VMEM((8, channels // width, columns[FINE], width), jnp.float32)]
    scratch += [pltpu.VMEM((conv_weight.shape[0], 9 * channels, channels), jnp.bfloat16),
                pltpu.VMEM(out_weight.shape, jnp.bfloat16)]
    for level in (FINE, SECOND):
        scratch += [rows_of(extents[level], level, 2), rows_of(extents[level] - 2, level, 2),
                    rows_of(extents[level] - 4, level), rows_of(extents[level] - 4, level)]
    scratch += [rows_of(extents[THIRD], THIRD, 2), rows_of(extents[THIRD] - 2, THIRD, 2)]
    scratch += [rows_of(extents[SECOND] - 8, SECOND),
                rows_of(extents[THIRD] - 4, THIRD)]
    scratch += [rows_of(max(extents[SECOND] - 8, extents[THIRD] - 4), SECOND, 0, jnp.float32)]
    scratch += [dma((copies,)) for _ in range(4)] + [dma((pairs,)) for _ in range(4)] + [dma((conv_weight.shape[0],)), dma]
    vmem, anywhere = pl.BlockSpec(memory_space=pltpu.VMEM), pl.BlockSpec(memory_space=pl.ANY)
    refined = pl.pallas_call(
        functools.partial(kernel, devices),
        out_shape=jax.ShapeDtypeStruct((extents[FINE] - 8, steps[FINE], LANES, channels), jnp.bfloat16),
        in_specs=[vmem, vmem, vmem, anywhere, vmem, anywhere, vmem],
        out_specs=vmem,
        scratch_shapes=scratch,
        compiler_params=pltpu.CompilerParams(
            collective_id=0, has_side_effects=True, vmem_limit_bytes=60 * 1024 * 1024),
    )(*fields, conv_weight.reshape(conv_weight.shape[0], 9 * channels, channels), conv_bias,
      out_weight, out_bias)
    per = 2 if blocks[FINE] % 2 == 0 else 1
    last = out_weight.shape[0] - 1
    return pl.pallas_call(
        functools.partial(lift_kernel, devices, last),
        grid=(blocks[FINE] // per,),
        out_shape=jax.ShapeDtypeStruct((2 * blocks[FINE], 2 * columns[FINE], channels), jnp.bfloat16),
        in_specs=[vmem, pl.BlockSpec((1, channels, channels), lambda g: (last, 0, 0)), vmem],
        out_specs=pl.BlockSpec((2 * per, 2 * columns[FINE], channels), lambda g: (g, 0, 0)),
        scratch_shapes=[
            pltpu.VMEM(refined.shape, jnp.float32),
            pltpu.VMEM((2 * per, channels // width, 2 * columns[FINE], width), jnp.float32),
        ],
    )(refined, out_weight, out_bias)


def solution(mesh):
    rows = P(("img", "rows"), None, None)
    return jax.shard_map(
        functools.partial(local, mesh.shape["rows"]),
        mesh=mesh,
        in_specs=(rows, rows, rows, P(), P(), P(), P()),
        out_specs=rows,
        check_vma=False,
    )
```

profile of v0, /device:TPU:4, one launch (start us, length us, event | category | flops | bytes accessed | tf_op | source)
XLA Modules:
  0.0 38.0 jit_solution(7062573663664589616)
XLA Ops:
  0.0 33.1 %shard_map.73.refined_ref = bf16[10,8,16,256]{3,2,1,0:T(8,128)(2,1)} custom-call(bf16[8,128,256]{2,1,0:T(8,128)(2,1)} %fine_ref.1, bf16[4,64,256]{2,1,0:T(8,128)(2,1)} %second_ref.1, bf16[2,32,256]{2,1,0:T(8,128)(2,1)} %third_ref.1, bf16[10,2304,256]{2,1,0:T(8,128)(2,1)} %bitcast.1, f32[10,256]{1,0:T(8,128)} %bias_ref.2, bf16[3,256,256]{2,1,0:T(8,128)(2,1)} %proj_ref.1, ...), custom_call_target="tpu_custom_call" | custom-call | tf_op jit(solution)/shard_map/pallas_call | solution.py:417
  33.1 4.9 %shard_map.74 = bf16[16,256,256]{2,1,0:T(8,128)(2,1)} custom-call(bf16[10,8,16,256]{3,2,1,0:T(8,128)(2,1)} %shard_map.73.refined_ref, bf16[3,256,256]{2,1,0:T(8,128)(2,1)} %proj_ref.1, f32[3,256]{1,0:T(4,128)} %bias_ref.3), custom_call_target="tpu_custom_call" | custom-call | tf_op jit(solution)/shard_map/pallas_call | solution.py:429
where the time goes:
time: 38.1 us; the launch traced here: 38 us
  Pallas kernels  38 us (100%)
    pallas_call x1, Pallas kernels, local(): pl.pallas_call(functools.partial(kernel, devices), out_shape=jax.ShapeDty...  33.1 us
    pallas_call x1, Pallas kernels, local(): pl.pallas_call(functools.partial(lift_kernel, devices, last), grid=(block...  4.86 us

commit v1 on v0

--- a/solution.py
+++ b/solution.py
@@ -9,6 +9,7 @@
 
 MESH = pl.DeviceIdType.MESH
 LANES = 16
+VMEM_MIB = 44
 FINE, SECOND, THIRD = 0, 1, 2
 HALOS = (5, 6, 5)
 WEIGHT_ORDER = (6, 0, 1, 2, 3, 4, 5, 7, 8, 9)
@@ -42,13 +43,14 @@
 
 
 def kernel(
-    devices, fine_ref, second_ref, third_ref, conv_hbm, bias_ref, proj_hbm, proj_bias_ref, refined_f,
+    devices, fine_hbm, second_hbm, third_hbm, conv_hbm, bias_hbm, proj_hbm, proj_bias_hbm, lines_f, table,
+    fine_ref, second_ref, third_ref, bias_ref, proj_bias_ref,
     fine_up, fine_down, second_up, second_down, third_up, third_down,
     fine_peer, fine_far, second_peer, second_far, fine_x, second_x, third_x, stage,
     weights, projs, padded_f, hidden_f, merged_f, path_f, padded_s, hidden_s, merged_s, path_s,
-    padded_t, hidden_t, refined_s, refined_t, proj_y,
+    padded_t, hidden_t, refined_f, refined_s, refined_t, proj_y,
     up_send, up_recv, down_send, down_recv,
-    pair_send, pair_recv, far_send, far_recv, weight_sem, proj_sem,
+    pair_send, pair_recv, far_send, far_recv, weight_sem, proj_sem, in_sem,
 ):
     me = lax.axis_index("rows")
     own = (fine_ref, second_ref, third_ref)
@@ -66,6 +68,14 @@
     source = me - 2 + 4 * odd
     reach = max(distance for _, distance, _ in plan)
 
+    in_copies = [
+        pltpu.make_async_copy(source, into, in_sem.at[at])
+        for at, (source, into) in enumerate((
+            (third_hbm, third_ref), (second_hbm, second_ref), (fine_hbm, fine_ref),
+            (bias_hbm, bias_ref), (proj_bias_hbm, proj_bias_ref)))
+    ]
+    for copy in in_copies:
+        copy.start()
     weight_copies = {
         k: pltpu.make_async_copy(conv_hbm.at[k], weights.at[k], weight_sem.at[k])
         for k in WEIGHT_ORDER
@@ -87,6 +97,8 @@
             pl.semaphore_signal(barrier, inc=1, device_id={"rows": me + distance}, device_id_type=MESH)
     expected = jnp.minimum(me, reach) + jnp.minimum(devices - 1 - me, reach)
     pl.semaphore_wait(barrier, expected)
+    for copy in in_copies:
+        copy.wait()
 
     up_copies, down_copies = [], []
     for at, (level, distance, rows) in enumerate(plan):
@@ -264,6 +276,7 @@
                 ref[row - first, 2 * t + 1] = high[t]
         return emit
 
+    fill_table(table, own[FINE].shape[1])
     halo_f, halo_s, halo_t = HALOS
     block_f, block_s, block_t = blocks
     take_rows(FINE, padded_f, 0, block_f)
@@ -334,6 +347,17 @@
     take_rows(FINE, padded_f, block_f, block_f + halo_f)
     join(FINE, halo_f, padded_f, hidden_f, merged_f, path_f, refined_f, 6,
          (halo_f, halo_f + block_f - 2))
+    count, steps_f = refined_f.shape[0], refined_f.shape[1]
+    last_bias = proj_bias_ref[projs.shape[0] - 1:projs.shape[0], :]
+    for r in range(0, count, count // 2):
+        rows = count // 2
+        y = jnp.dot(refined_f[r:r + rows].reshape(rows * steps_f * LANES, -1), projs[projs.shape[0] - 1],
+                    preferred_element_type=jnp.float32) + last_bias
+        lines_f[r:r + rows] = y.astype(jnp.bfloat16).reshape(rows, steps_f, LANES, -1)
+    lines_f[0] = jnp.where(me == 0, lines_f[1].astype(jnp.float32), lines_f[0].astype(jnp.float32)).astype(jnp.bfloat16)
+    lines_f[count - 1] = jnp.where(
+        me == devices - 1, lines_f[count - 2].astype(jnp.float32),
+        lines_f[count - 1].astype(jnp.float32)).astype(jnp.bfloat16)
 
     for at, (_, distance, _) in enumerate(plan):
         pl.when(me + distance < devices)(up_copies[at].wait_send)
@@ -345,39 +369,35 @@
             pl.when(has_target)(copy.wait_send)
 
 
-def lift_kernel(devices, index, refined_ref, proj_ref, bias_ref, out_ref, lines, stage):
-    me = lax.axis_index("rows")
+def fill_table(table, columns):
+    steps = columns // LANES
+    wide = 2 * columns
+    for half in range(2):
+        for side in range(2):
+            out = lax.broadcasted_iota(jnp.int32, (wide, columns), 0)
+            place = lax.broadcasted_iota(jnp.int32, (wide, columns), 1)
+            column = (place % LANES) * steps + place // LANES
+            near = out // 2
+            far = jnp.clip(near + 2 * (out % 2) - 1, 0, columns - 1)
+            weight = jnp.where(column == near, 0.75, 0.0) + jnp.where(column == far, 0.25, 0.0)
+            weight = weight * (0.75 if half == side else 0.25)
+            table[half * wide:(half + 1) * wide, side * columns:(side + 1) * columns] = weight.astype(jnp.bfloat16)
+
+
+def lift_kernel(lines_ref, table_ref, out_ref):
     at = pl.program_id(0)
-    count, steps = refined_ref.shape[0], refined_ref.shape[1]
+    steps, channels = lines_ref.shape[1], lines_ref.shape[3]
+    columns = steps * LANES
+    wide = 2 * columns
     per = out_ref.shape[0] // 2
-    channels = refined_ref.shape[3]
-    width = stage.shape[3]
-
-    @pl.when(at == 0)
-    def _():
-        for m in range(0, count, 2):
-            rows = min(2, count - m)
-            y = jnp.dot(refined_ref[m:m + rows].reshape(rows * steps * LANES, channels), proj_ref[0],
-                        preferred_element_type=jnp.float32)
-            lines[m:m + rows] = y.reshape(rows, steps, LANES, channels)
-        lines[0] = jnp.where(me == 0, lines[1], lines[0])
-        lines[count - 1] = jnp.where(me == devices - 1, lines[count - 2], lines[count - 1])
-
-    bias = bias_ref[index:index + 1, :]
-    for i in range(per):
-        m = 1 + at * per + i
-        for half in range(2):
-            row = 0.75 * lines[m] + 0.25 * lines[m - 1 + 2 * half] + bias
-            before, after = edge_steps(row[None], True)
-            for t in range(steps):
-                low = 0.25 * (row[t - 1] if t else before[0]) + 0.75 * row[t]
-                high = 0.75 * row[t] + 0.25 * (row[t + 1] if t < steps - 1 else after[0])
-                for c in range(channels // width):
-                    part = slice(c * width, (c + 1) * width)
-                    stage[2 * i + half, c, pl.ds(2 * t, LANES, stride=2 * steps), :] = low[:, part]
-                    stage[2 * i + half, c, pl.ds(2 * t + 1, LANES, stride=2 * steps), :] = high[:, part]
-            for c in range(channels // width):
-                out_ref[2 * i + half, :, c * width:(c + 1) * width] = stage[2 * i + half, c].astype(jnp.bfloat16)
+    for i in range(per + 1):
+        pair = lines_ref[pl.ds(at * per + i, 2)].reshape(2 * columns, channels)
+        first, last = (wide if i == 0 else 0), (wide if i == per else 2 * wide)
+        rows = jnp.dot(table_ref[first:last], pair, preferred_element_type=jnp.float32).astype(jnp.bfloat16)
+        if i > 0:
+            out_ref[2 * i - 1] = rows[0:wide]
+        if i < per:
+            out_ref[2 * i] = rows[last - first - wide:]
 
 
 def local(devices, feat_fine, feat_second, feat_third, conv_weight, conv_bias, out_weight, out_bias):
@@ -398,7 +418,9 @@
     copies = len(direct_sends(blocks))
     pairs = sum(len(pair_chunks(level, blocks[level])) for level in (FINE, SECOND))
     dma = pltpu.SemaphoreType.DMA
-    scratch = [raw(HALOS[level], level) for level in range(3) for _ in range(2)]
+    scratch = [raw(blocks[level], level) for level in range(3)]
+    scratch += [pltpu.VMEM(conv_bias.shape, jnp.float32), pltpu.VMEM(out_bias.shape, jnp.float32)]
+    scratch += [raw(HALOS[level], level) for level in range(3) for _ in range(2)]
     for level in (FINE, SECOND):
         scratch += [raw(blocks[level], level), raw(min(blocks[level], HALOS[level]), level)]
     scratch += [rows_of(extents[level], level) for level in range(3)]
@@ -409,34 +431,32 @@
         scratch += [rows_of(extents[level], level, 2), rows_of(extents[level] - 2, level, 2),
                     rows_of(extents[level] - 4, level), rows_of(extents[level] - 4, level)]
     scratch += [rows_of(extents[THIRD], THIRD, 2), rows_of(extents[THIRD] - 2, THIRD, 2)]
-    scratch += [rows_of(extents[SECOND] - 8, SECOND),
+    scratch += [rows_of(extents[FINE] - 8, FINE), rows_of(extents[SECOND] - 8, SECOND),
                 rows_of(extents[THIRD] - 4, THIRD)]
     scratch += [rows_of(max(extents[SECOND] - 8, extents[THIRD] - 4), SECOND, 0, jnp.float32)]
-    scratch += [dma((copies,)) for _ in range(4)] + [dma((pairs,)) for _ in range(4)] + [dma((conv_weight.shape[0],)), dma]
-    vmem, anywhere = pl.BlockSpec(memory_space=pltpu.VMEM), pl.BlockSpec(memory_space=pl.ANY)
-    refined = pl.pallas_call(
+    scratch += [dma((copies,)) for _ in range(4)] + [dma((pairs,)) for _ in range(4)] + [dma((conv_weight.shape[0],)), dma, dma((5,))]
+    vmem, far = pl.BlockSpec(memory_space=pltpu.VMEM), pl.BlockSpec(memory_space=pltpu.HBM)
+    wide = 2 * columns[FINE]
+    lines, table = pl.pallas_call(
         functools.partial(kernel, devices),
-        out_shape=jax.ShapeDtypeStruct((extents[FINE] - 8, steps[FINE], LANES, channels), jnp.bfloat16),
-        in_specs=[vmem, vmem, vmem, anywhere, vmem, anywhere, vmem],
-        out_specs=vmem,
+        out_shape=[jax.ShapeDtypeStruct((extents[FINE] - 8, steps[FINE], LANES, channels), jnp.bfloat16),
+                   jax.ShapeDtypeStruct((2 * wide, 2 * columns[FINE]), jnp.bfloat16)],
+        in_specs=[far] * 7,
+        out_specs=[vmem, vmem],
         scratch_shapes=scratch,
         compiler_params=pltpu.CompilerParams(
-            collective_id=0, has_side_effects=True, vmem_limit_bytes=60 * 1024 * 1024),
-    )(*fields, conv_weight.reshape(conv_weight.shape[0], 9 * channels, channels), conv_bias,
-      out_weight, out_bias)
+            collective_id=0, has_side_effects=True, vmem_limit_bytes=VMEM_MIB * 1024 * 1024),
+    )(*[pltpu.with_memory_space_constraint(v, pltpu.HBM) for v in (
+        *fields, conv_weight.reshape(conv_weight.shape[0], 9 * channels, channels), conv_bias, out_weight, out_bias)])
     per = 2 if blocks[FINE] % 2 == 0 else 1
-    last = out_weight.shape[0] - 1
     return pl.pallas_call(
-        functools.partial(lift_kernel, devices, last),
+        lift_kernel,
         grid=(blocks[FINE] // per,),
-        out_shape=jax.ShapeDtypeStruct((2 * blocks[FINE], 2 * columns[FINE], channels), jnp.bfloat16),
-        in_specs=[vmem, pl.BlockSpec((1, channels, channels), lambda g: (last, 0, 0)), vmem],
-        out_specs=pl.BlockSpec((2 * per, 2 * columns[FINE], channels), lambda g: (g, 0, 0)),
-        scratch_shapes=[
-            pltpu.VMEM(refined.shape, jnp.float32),
-            pltpu.VMEM((2 * per, channels // width, 2 * columns[FINE], width), jnp.float32),
-        ],
-    )(refined, out_weight, out_bias)
+        out_shape=jax.ShapeDtypeStruct((2 * blocks[FINE], wide, channels), jnp.bfloat16),
+        in_specs=[vmem, vmem],
+        out_specs=pl.BlockSpec((2 * per, wide, channels), lambda g: (g, 0, 0)),
+        compiler_params=pltpu.CompilerParams(vmem_limit_bytes=8 * 1024 * 1024),
+    )(lines, table)
 
 
 def solution(mesh):

time: 38.1 us -> 35.8 us (0.940)
  Pallas kernels: 38 us -> 35.4 us
    pallas_call x2, Pallas kernels: 38 us -> 35.4 us  [the longest x1 32.9 us: local(): pl.pallas_call(functools.partial(kernel, devices), out_shape=[jax.ShapeDt...]
where the time goes in v1:
time: 35.8 us; the launch traced here: 35.5 us
  Pallas kernels  35.4 us (99%)
    pallas_call x1, Pallas kernels, local(): pl.pallas_call(functools.partial(kernel, devices), out_shape=[jax.ShapeDt...  32.9 us
    pallas_call x1, Pallas kernels, local(): pl.pallas_call(lift_kernel, grid=(blocks[FINE] // per,), out_shape=jax.Sh...  2.53 us

profile of v1, /device:TPU:4, one launch (start us, length us, event | category | flops | bytes accessed | tf_op | source)
XLA Modules:
  0.0 35.5 jit_solution(11653080198477073082)
XLA Ops:
  0.0 32.9 %shard_map.73 = (bf16[10,8,16,256]{3,2,1,0:T(8,128)(2,1)S(1)}, bf16[512,256]{1,0:T(8,128)(2,1)S(1)}) custom-call(bf16[8,128,256]{2,1,0:T(8,128)(2,1)} %fine_hbm.1, bf16[4,64,256]{2,1,0:T(8,128)(2,1)} %second_hbm.1, bf16[2,32,256]{2,1,0:T(8,128)(2,1)} %third_hbm.1, bf16[10,2304,256]{2,1,0:T(8,128)(2,1)} %bitcast.1, f32[10,256]{1,0:T(8,128)} %bias_hbm.1, ...), custom_call_target="tpu_custom_call" | custom-call | tf_op jit(solution)/shard_map/pallas_call | solution.py:440
  32.9 2.5 %shard_map.74 = bf16[16,256,256]{2,1,0:T(8,128)(2,1)} custom-call(bf16[10,8,16,256]{3,2,1,0:T(8,128)(2,1)S(1)} %get-tuple-element.7.lines_ref, bf16[512,256]{1,0:T(8,128)(2,1)S(1)} %get-tuple-element.8.table_ref), custom_call_target="tpu_custom_call" | custom-call | tf_op jit(solution)/shard_map/pallas_call | solution.py:452

commit v2 on v1

v2 whole, which is shorter than its diff:
```python
import functools

import jax
import jax.numpy as jnp
from jax import lax
from jax.experimental import pallas as pl
from jax.experimental.pallas import tpu as pltpu
from jax.sharding import PartitionSpec as P

MESH = pl.DeviceIdType.MESH
LANES = 16
VMEM_MIB = 44
MOST = 640
RING = 2
FINE, SECOND, THIRD = 0, 1, 2
HALOS = (5, 6, 5)
WEIGHT_ORDER = (6, 7, 2, 0, 1, 3, 4, 5, 8, 9)


def direct_rows(level, block):
    halo = HALOS[level]
    return [(d, min(block, halo - (d - 1) * block)) for d in range(2, -(-halo // block) + 1)]


def pair_rows(level, block):
    near = min(block, HALOS[level])
    if level == THIRD:
        return [(0, block, True)]
    if level == SECOND:
        cuts = [block, block // 2, 0] if block > 1 else [block, 0]
        return [(low, high - low, True) for high, low in zip(cuts, cuts[1:])]
    away, beside = list(range(block - 1, -1, -1)), list(range(block))
    order = away[:RING] + beside[:RING] + away[RING:near]
    order = list(dict.fromkeys(order + beside[:near] + away))
    return [(r, 1, r >= block - near) for r in order]


def pairs_of(first, last, most):
    rows = last - first
    parts = min(rows, 2 * -(-rows // (2 * most)))
    cuts = [first + rows * i // parts for i in range(parts + 1)]
    return [(p, q - p) for p, q in zip(cuts, cuts[1:])]


def edge_steps(values, clamp):
    steps = values.shape[1]
    first, last = values[:, 0], values[:, steps - 1]
    place = lax.broadcasted_iota(jnp.int32, first.shape, 1)
    zero = jnp.zeros_like(first)
    before = jnp.where(place == 0, first if clamp else zero, pltpu.roll(last, 1, 1))
    after = jnp.where(place == LANES - 1, last if clamp else zero, pltpu.roll(first, LANES - 1, 1))
    return before, after


def kernel(
    devices, fine_hbm, second_hbm, third_hbm, conv_hbm, bias_hbm, proj_hbm, proj_bias_hbm, lines_f, table,
    fine_ref, second_ref, third_ref, bias_ref, proj_bias_ref,
    fine_other, second_other, third_other,
    second_up, second_down, third_up, third_down,
    fine_x, second_x, third_x, stage, weights, projs,
    padded_f, hidden_f, addend_f, joined_f, hidden2_f, merged_f, path_f,
    padded_s, hidden_s, merged_s, path_s,
    padded_t, hidden_t, refined_f, refined_s, refined_t, proj_y,
    up_send, up_recv, down_send, down_recv, up2_send, down2_send,
    pair_send, pair_recv, far_send, far_recv, weight_sem, proj_sem, in_sem,
):
    me = lax.axis_index("rows")
    own = (fine_ref, second_ref, third_ref)
    ups = (None, second_up, third_up)
    downs = (None, second_down, third_down)
    blocks = tuple(ref.shape[0] for ref in own)
    fields = (fine_x, second_x, third_x)
    others = (fine_other, second_other, third_other)
    odd = me % 2
    even = odd == 0
    is_odd = odd == 1
    partner = me + 1 - 2 * odd
    target = me + 2 - 4 * odd
    source = me - 2 + 4 * odd

    in_copies = [
        pltpu.make_async_copy(source_ref, into, in_sem.at[at])
        for at, (source_ref, into) in enumerate((
            (second_hbm, second_ref), (third_hbm, third_ref), (fine_hbm, fine_ref),
            (bias_hbm, bias_ref), (proj_bias_hbm, proj_bias_ref)))
    ]
    for copy in in_copies:
        copy.start()
    weight_copies = {
        k: pltpu.make_async_copy(conv_hbm.at[k], weights.at[k], weight_sem.at[k])
        for k in WEIGHT_ORDER
    }
    proj_copy = pltpu.make_async_copy(proj_hbm, projs, proj_sem)
    for at, k in enumerate(WEIGHT_ORDER):
        weight_copies[k].start()
        if at == 3:
            proj_copy.start()

    reach = max([2] + [d for level in (SECOND, THIRD) for d, _ in direct_rows(level, blocks[level])])
    barrier = pltpu.get_barrier_semaphore()
    for distance in range(1, reach + 1):
        @pl.when(me >= distance)
        def _():
            pl.semaphore_signal(barrier, inc=1, device_id={"rows": me - distance}, device_id_type=MESH)

        @pl.when(me + distance < devices)
        def _():
            pl.semaphore_signal(barrier, inc=1, device_id={"rows": me + distance}, device_id_type=MESH)
    expected = jnp.minimum(me, reach) + jnp.minimum(devices - 1 - me, reach)
    pl.semaphore_wait(barrier, expected)
    for copy in in_copies:
        copy.wait()

    has_target = jnp.logical_and(target >= 0, target < devices)
    has_source = jnp.logical_and(source >= 0, source < devices)

    def remote(src, dst, send, recv, device):
        return pltpu.make_async_remote_copy(
            src_ref=src, dst_ref=dst, send_sem=send, recv_sem=recv,
            device_id={"rows": device}, device_id_type=MESH)

    starts, sends, arrivals, relays = [], [], {THIRD: [], SECOND: []}, {THIRD: [], SECOND: []}
    serial = 0
    for level in (THIRD, SECOND):
        block, halo = blocks[level], HALOS[level]
        for distance, rows in direct_rows(level, block):
            at = serial
            serial += 1
            up_src, up_dst = pl.ds(block - rows, rows), pl.ds(halo - (distance - 1) * block - rows, rows)
            down_src, down_dst = pl.ds(0, rows), pl.ds((distance - 1) * block, rows)
            up = remote(own[level].at[up_src], ups[level].at[up_dst], up_send.at[at], up_recv.at[at], me + distance)
            down = remote(
                own[level].at[down_src], downs[level].at[down_dst], down_send.at[at], down_recv.at[at], me - distance)
            up_ok, down_ok = me + distance < devices, me >= distance
            arrivals[level] += [(down_ok, up), (up_ok, down)]
            if distance % 2 == 0:
                starts += [(level, up_ok, up), (level, down_ok, down)]
                sends += [(up_ok, up), (down_ok, down)]
                continue
            up_ok, down_ok = jnp.logical_and(is_odd, up_ok), jnp.logical_and(even, down_ok)
            starts += [(level, up_ok, up), (level, down_ok, down)]
            sends += [(up_ok, up), (down_ok, down)]
            hop = distance - 1
            up2 = remote(
                others[level].at[up_src], ups[level].at[up_dst], up2_send.at[at], up_recv.at[at], me + hop)
            down2 = remote(
                others[level].at[down_src], downs[level].at[down_dst], down2_send.at[at], down_recv.at[at], me - hop)
            up2_ok = jnp.logical_and(is_odd, me + hop < devices)
            down2_ok = jnp.logical_and(even, me >= hop)
            relays[level] += [(up2_ok, up2), (down2_ok, down2)]
            sends += [(up2_ok, up2), (down2_ok, down2)]

    pair_copies, far_copies = {}, {}
    serial = 0
    for level in (SECOND, THIRD, FINE):
        block = blocks[level]
        near = min(block, HALOS[level])
        pair_copies[level], far_copies[level] = [], []
        for row, rows, forwarded in pair_rows(level, block):
            mirrored = block - row - rows
            at = mirrored + odd * (row - mirrored)
            pair_copies[level].append(remote(
                own[level].at[pl.ds(at, rows)], others[level].at[pl.ds(at, rows)],
                pair_send.at[serial], pair_recv.at[serial], partner))
            relay = None
            if forwarded:
                held = row + odd * (mirrored - row)
                spot = block + held - (1 - odd) * (block - near)
                relay = remote(
                    others[level].at[pl.ds(held, rows)], others[level].at[pl.ds(spot, rows)],
                    far_send.at[serial], far_recv.at[serial], target)
            far_copies[level].append(relay)
            serial += 1
        for wanted, ok, copy in starts:
            if wanted == level:
                pl.when(ok)(copy.start)
        for copy in pair_copies[level]:
            copy.start()

    def pass_on(level, chunk):
        pair_copies[level][chunk].wait_recv()
        if far_copies[level][chunk] is not None:
            pl.when(has_target)(far_copies[level][chunk].start)
        for ok, copy in relays.get(level, ()):
            pl.when(ok)(copy.start)

    def arrive(level):
        for ok, copy in arrivals[level]:
            pl.when(ok)(copy.wait_recv)
        for copy in far_copies[level]:
            pl.when(has_source)(copy.wait_recv)

    def inside(level, row):
        block = blocks[level]
        if 0 <= row < block:
            return None
        place = me * block + row
        return jnp.logical_and(place >= 0, place < devices * block)

    def store_padded(ref, at, values, level, first_row):
        steps = values.shape[1]
        for r in range(values.shape[0]):
            row = values[r:r + 1].astype(jnp.float32)
            valid = inside(level, first_row + r)
            if valid is not None:
                row = jnp.where(valid, row, 0.0)
            before, after = edge_steps(row, False)
            ref[at + r, 1:steps + 1] = row[0].astype(jnp.bfloat16)
            ref[at + r, 0] = before[0].astype(jnp.bfloat16)
            ref[at + r, steps + 1] = after[0].astype(jnp.bfloat16)

    def conv(ref, k, tiles, emit):
        steps = ref.shape[1] - 2
        for r, rows in tiles:
            flat = jnp.concatenate(
                [ref[r + a:r + a + rows, b:b + steps].reshape(rows * steps * LANES, -1)
                 for a in range(3) for b in range(3)], axis=1)
            acc = jnp.dot(flat, weights[k], preferred_element_type=jnp.float32)
            acc = acc + bias_ref[k:k + 1, :]
            emit(r, acc.reshape(rows, steps, LANES, -1))

    def tiles_of(level, first, last):
        return pairs_of(first, last, max(1, MOST // own[level].shape[1]))

    def raw_row(level, place):
        block, halo = blocks[level], HALOS[level]
        near = min(block, halo)
        if 0 <= place < block:
            return own[level][place]
        if place < 0:
            j = -1 - place
            if j >= block:
                return ups[level][halo - 1 - j]
            return others[level][block - 1 - j + (1 - odd) * near]
        j = place - block
        if j >= block:
            return downs[level][j]
        return others[level][j + odd * block]

    def take_rows(level, padded, first, last):
        halo = HALOS[level]
        columns = own[level].shape[1]
        steps = columns // LANES
        width = stage.shape[3]
        for place in range(first, last):
            row = raw_row(level, place).astype(jnp.float32)
            slot = place % stage.shape[0]
            parts = range(row.shape[1] // width)
            for c in parts:
                stage[slot, c, 0:columns] = row[:, c * width:(c + 1) * width]
            turned = jnp.concatenate(
                [jnp.concatenate([stage[slot, c, pl.ds(t, LANES, stride=steps), :] for c in parts], axis=1)[None]
                 for t in range(steps)], axis=0)
            fields[level][halo + place] = turned.astype(jnp.bfloat16)
            store_padded(padded, halo + place, jnp.maximum(turned, 0.0)[None], level, place)

    def hidden(level, source, target, k, tiles, row0):
        def emit(r, acc):
            store_padded(target, r, jnp.maximum(acc, 0.0), level, row0 + r)
        conv(source, k, tiles, emit)

    def source_rows(level, row, rows):
        at = HALOS[level] + row
        return fields[level][at:at + rows].astype(jnp.float32)

    def lift(level, refined, halo, index, emit, extra):
        count, steps = refined.shape[0], refined.shape[1]
        block = blocks[level]
        w = projs[index]
        tile = max(1, 512 // (steps * LANES))
        for r in range(0, count, tile):
            rows = min(tile, count - r)
            y = jnp.dot(refined[r:r + rows].reshape(rows * steps * LANES, -1), w,
                        preferred_element_type=jnp.float32)
            proj_y[r:r + rows, 0:steps] = y.reshape(rows, steps, LANES, -1)

        def line(m):
            value = proj_y[m, 0:steps]
            before, after = halo - 1 - m, m - halo - block
            if before >= 0 and before % block == 0:
                value = jnp.where(me == before // block, proj_y[m + 1, 0:steps], value)
            if after >= 0 and after % block == 0:
                value = jnp.where(me == devices - 1 - after // block, proj_y[m - 1, 0:steps], value)
            return value

        bias = proj_bias_ref[index:index + 1, :]

        def columns(out_row, major, minor):
            row = (0.75 * major + 0.25 * minor + bias)[None]
            before, after = edge_steps(row, True)
            wide = jnp.concatenate([before[:, None], row, after[:, None]], axis=1)[0]
            low = 0.25 * wide[0:steps] + 0.75 * row[0]
            high = 0.75 * row[0] + 0.25 * wide[2:steps + 2]
            emit(out_row, low.astype(jnp.bfloat16), high.astype(jnp.bfloat16))

        for m in range(count):
            even = 2 * (m - halo)
            if 1 <= m and (m < count - 1 or extra):
                columns(even, line(m), line(m - 1))
            if m < count - 1 and (m >= 1 or extra):
                columns(even + 1, line(m), line(m + 1))

    def emit_to(ref, first):
        def emit(row, low, high):
            for t in range(low.shape[0]):
                ref[row - first, 2 * t] = low[t]
                ref[row - first, 2 * t + 1] = high[t]
        return emit

    halo_f, halo_s, halo_t = HALOS
    block_f, block_s, block_t = blocks
    order = [row for row, _, _ in pair_rows(FINE, block_f)]

    def fine_unit(tiles):
        def emit(r, acc):
            rows = acc.shape[0]
            addend_f[r:r + rows] = acc + source_rows(FINE, r + 2 - halo_f, rows)
        conv(hidden_f, 7, tiles, emit)

    def fine_join(first, last):
        for r in range(first, last):
            total = (addend_f[r:r + 1] + path_f[r:r + 1].astype(jnp.float32)).astype(jnp.bfloat16)
            merged_f[r:r + 1] = total
            store_padded(joined_f, r, jnp.maximum(total, 0), FINE, r + 2 - halo_f)

    def fine_refined(tiles):
        def emit(r, acc):
            rows = acc.shape[0]
            refined_f[r:r + rows] = (acc + merged_f[r + 2:r + 2 + rows].astype(jnp.float32)).astype(jnp.bfloat16)
        conv(hidden2_f, 9, tiles, emit)

    last_index = projs.shape[0] - 1

    def project(tiles):
        bias = proj_bias_ref[last_index:last_index + 1, :]
        for r, rows in tiles:
            y = jnp.dot(refined_f[r:r + rows].reshape(rows * refined_f.shape[1] * LANES, -1), projs[last_index],
                        preferred_element_type=jnp.float32) + bias
            lines_f[r:r + rows] = y.astype(jnp.bfloat16).reshape(rows, refined_f.shape[1], LANES, -1)

    take_rows(FINE, padded_f, 0, block_f)
    weight_copies[6].wait()
    hidden(FINE, padded_f, hidden_f, 6, tiles_of(FINE, halo_f, halo_f + block_f - 2), 1 - halo_f)
    weight_copies[7].wait()
    fine_unit(tiles_of(FINE, halo_f, halo_f + block_f - 4))
    for at in range(len(pair_copies[SECOND])):
        pass_on(SECOND, at)
    take_rows(THIRD, padded_t, 0, block_t)
    take_rows(SECOND, padded_s, 0, block_s)
    fill_table(table, own[FINE].shape[1])
    pass_on(THIRD, 0)

    last_s = block_s + 2 * halo_s
    arrive(SECOND)
    pass_on(FINE, 0)
    take_rows(SECOND, padded_s, -halo_s, 0)
    take_rows(SECOND, padded_s, block_s, block_s + halo_s)
    weight_copies[2].wait()
    hidden(SECOND, padded_s, hidden_s, 2, tiles_of(SECOND, 0, last_s - 2), 1 - halo_s)
    arrive(THIRD)
    pass_on(FINE, 1)
    take_rows(THIRD, padded_t, -halo_t, 0)
    take_rows(THIRD, padded_t, block_t, block_t + halo_t)
    weight_copies[0].wait()
    weight_copies[1].wait()
    weight_copies[3].wait()
    proj_copy.wait()
    hidden(THIRD, padded_t, hidden_t, 0, tiles_of(THIRD, 0, block_t + 2 * halo_t - 2), 1 - halo_t)

    def emit_third(r, acc):
        rows = acc.shape[0]
        total = acc + source_rows(THIRD, r + 2 - halo_t, rows)
        refined_t[r:r + rows] = total.astype(jnp.bfloat16)

    conv(hidden_t, 1, tiles_of(THIRD, 0, block_t + 2 * halo_t - 4), emit_third)
    lift(THIRD, refined_t, halo_t - 2, 0, emit_to(path_s, 2 - halo_s), False)

    def emit_merged(r, acc):
        rows = acc.shape[0]
        total = acc + source_rows(SECOND, r + 2 - halo_s, rows) + path_s[r:r + rows].astype(jnp.float32)
        total = total.astype(jnp.bfloat16)
        merged_s[r:r + rows] = total
        store_padded(padded_s, r, jnp.maximum(total, 0), SECOND, r + 2 - halo_s)

    conv(hidden_s, 3, tiles_of(SECOND, 0, last_s - 4), emit_merged)
    pass_on(FINE, 2)
    pass_on(FINE, 3)

    weight_copies[4].wait()
    weight_copies[5].wait()
    hidden(SECOND, padded_s, hidden_s, 4, tiles_of(SECOND, 0, last_s - 6), 3 - halo_s)

    def emit_refined(r, acc):
        rows = acc.shape[0]
        total = acc + merged_s[r + 2:r + 2 + rows].astype(jnp.float32)
        refined_s[r:r + rows] = total.astype(jnp.bfloat16)

    conv(hidden_s, 5, tiles_of(SECOND, 0, last_s - 8), emit_refined)
    pass_on(FINE, 4)

    ring = RING
    wide_f = block_f + 2 * halo_f
    far_of = {row: at for at, row in enumerate(order)}
    for d in range(ring):
        pl.when(has_source)(far_copies[FINE][far_of[block_f - 1 - d]].wait_recv)
    lift(SECOND, refined_s, halo_s - 4, 1, emit_to(path_f, 2 - halo_f), True)
    take_rows(FINE, padded_f, -ring, 0)
    take_rows(FINE, padded_f, block_f, block_f + ring)
    hidden(FINE, padded_f, hidden_f, 6, [(halo_f - ring, ring), (halo_f + block_f - 2, ring)], 1 - halo_f)
    fine_unit([(halo_f - ring, ring), (halo_f + block_f - 4, ring)])
    low, high = halo_f - 2, halo_f - 2 + block_f
    fine_join(low, high)
    pass_on(FINE, 5)
    weight_copies[8].wait()
    weight_copies[9].wait()
    hidden(FINE, joined_f, hidden2_f, 8, tiles_of(FINE, low, high - 2), 3 - halo_f)
    pass_on(FINE, 6)
    fine_refined(tiles_of(FINE, low, high - 4))
    project(tiles_of(FINE, low, high - 4))

    for at in range(7, len(order)):
        pass_on(FINE, at)
    for at, row in enumerate(order):
        if far_copies[FINE][at] is not None and row < block_f - ring:
            pl.when(has_source)(far_copies[FINE][at].wait_recv)
    take_rows(FINE, padded_f, -halo_f, -ring)
    take_rows(FINE, padded_f, block_f + ring, block_f + halo_f)
    edge = halo_f - ring
    ends = lambda count: [(0, edge), (count - edge, edge)]
    hidden(FINE, padded_f, hidden_f, 6, ends(wide_f - 2), 1 - halo_f)
    fine_unit(ends(wide_f - 4))
    fine_join(0, edge)
    fine_join(wide_f - 4 - edge, wide_f - 4)
    hidden(FINE, joined_f, hidden2_f, 8, ends(wide_f - 6), 3 - halo_f)
    fine_refined(ends(wide_f - 8))
    project(ends(wide_f - 8))
    count = lines_f.shape[0]
    for end, beside, at_end in ((0, 1, me == 0), (count - 1, count - 2, me == devices - 1)):
        lines_f[end] = jnp.where(
            at_end, lines_f[beside].astype(jnp.float32), lines_f[end].astype(jnp.float32)).astype(jnp.bfloat16)

    for ok, copy in sends:
        pl.when(ok)(copy.wait_send)
    for level in (THIRD, SECOND, FINE):
        for copy in pair_copies[level]:
            copy.wait_send()
        for copy in far_copies[level]:
            if copy is not None:
                pl.when(has_target)(copy.wait_send)


def fill_table(table, columns):
    steps = columns // LANES
    wide = 2 * columns
    for half in range(2):
        for side in range(2):
            out = lax.broadcasted_iota(jnp.int32, (wide, columns), 0)
            place = lax.broadcasted_iota(jnp.int32, (wide, columns), 1)
            column = (place % LANES) * steps + place // LANES
            near = out // 2
            far = jnp.clip(near + 2 * (out % 2) - 1, 0, columns - 1)
            weight = jnp.where(column == near, 0.75, 0.0) + jnp.where(column == far, 0.25, 0.0)
            weight = weight * (0.75 if half == side else 0.25)
            table[half * wide:(half + 1) * wide, side * columns:(side + 1) * columns] = weight.astype(jnp.bfloat16)


def lift_kernel(lines_ref, table_ref, out_ref):
    at = pl.program_id(0)
    steps, channels = lines_ref.shape[1], lines_ref.shape[3]
    columns = steps * LANES
    wide = 2 * columns
    per = out_ref.shape[0] // 2
    for i in range(per + 1):
        pair = lines_ref[pl.ds(at * per + i, 2)].reshape(2 * columns, channels)
        first, last = (wide if i == 0 else 0), (wide if i == per else 2 * wide)
        rows = jnp.dot(table_ref[first:last], pair, preferred_element_type=jnp.float32).astype(jnp.bfloat16)
        if i > 0:
            out_ref[2 * i - 1] = rows[0:wide]
        if i < per:
            out_ref[2 * i] = rows[last - first - wide:]


def local(devices, feat_fine, feat_second, feat_third, conv_weight, conv_bias, out_weight, out_bias):
    fields = (feat_fine, feat_second, feat_third)
    channels = feat_fine.shape[2]
    blocks = [v.shape[0] for v in fields]
    columns = [v.shape[1] for v in fields]
    steps = [c // LANES for c in columns]
    width = min(128, channels)

    def raw(count, level):
        return pltpu.VMEM((count, columns[level], channels), jnp.bfloat16)

    def rows_of(count, level, extra=0, dtype=jnp.bfloat16):
        return pltpu.VMEM((count, steps[level] + extra, LANES, channels), dtype)

    extents = [block + 2 * halo for block, halo in zip(blocks, HALOS)]
    copies = sum(len(direct_rows(level, blocks[level])) for level in (SECOND, THIRD))
    pairs = sum(len(pair_rows(level, blocks[level])) for level in range(3))
    dma = pltpu.SemaphoreType.DMA
    scratch = [raw(blocks[level], level) for level in range(3)]
    scratch += [pltpu.VMEM(conv_bias.shape, jnp.float32), pltpu.VMEM(out_bias.shape, jnp.float32)]
    for level in range(3):
        scratch += [raw(blocks[level] + min(blocks[level], HALOS[level]), level)]
    scratch += [raw(HALOS[level], level) for level in (SECOND, THIRD) for _ in range(2)]
    scratch += [rows_of(extents[level], level) for level in range(3)]
    scratch += [pltpu.VMEM((8, channels // width, columns[FINE], width), jnp.float32)]
    scratch += [pltpu.VMEM((conv_weight.shape[0], 9 * channels, channels), jnp.bfloat16),
                pltpu.VMEM(out_weight.shape, jnp.bfloat16)]
    scratch += [rows_of(extents[FINE], FINE, 2), rows_of(extents[FINE] - 2, FINE, 2),
                rows_of(extents[FINE] - 4, FINE, 0, jnp.float32), rows_of(extents[FINE] - 4, FINE, 2),
                rows_of(extents[FINE] - 6, FINE, 2), rows_of(extents[FINE] - 4, FINE), rows_of(extents[FINE] - 4, FINE)]
    scratch += [rows_of(extents[SECOND], SECOND, 2), rows_of(extents[SECOND] - 2, SECOND, 2),
                rows_of(extents[SECOND] - 4, SECOND), rows_of(extents[SECOND] - 4, SECOND)]
    scratch += [rows_of(extents[THIRD], THIRD, 2), rows_of(extents[THIRD] - 2, THIRD, 2)]
    scratch += [rows_of(extents[FINE] - 8, FINE), rows_of(extents[SECOND] - 8, SECOND),
                rows_of(extents[THIRD] - 4, THIRD)]
    scratch += [rows_of(max(extents[SECOND] - 8, extents[THIRD] - 4), SECOND, 0, jnp.float32)]
    scratch += [dma((copies,)) for _ in range(6)] + [dma((pairs,)) for _ in range(4)]
    scratch += [dma((conv_weight.shape[0],)), dma, dma((5,))]
    vmem, far = pl.BlockSpec(memory_space=pltpu.VMEM), pl.BlockSpec(memory_space=pltpu.HBM)
    wide = 2 * columns[FINE]
    lines, table = pl.pallas_call(
        functools.partial(kernel, devices),
        out_shape=[jax.ShapeDtypeStruct((extents[FINE] - 8, steps[FINE], LANES, channels), jnp.bfloat16),
                   jax.ShapeDtypeStruct((2 * wide, 2 * columns[FINE]), jnp.bfloat16)],
        in_specs=[far] * 7,
        out_specs=[vmem, vmem],
        scratch_shapes=scratch,
        compiler_params=pltpu.CompilerParams(
            collective_id=0, has_side_effects=True, vmem_limit_bytes=VMEM_MIB * 1024 * 1024),
    )(*[pltpu.with_memory_space_constraint(v, pltpu.HBM) for v in (
        *fields, conv_weight.reshape(conv_weight.shape[0], 9 * channels, channels), conv_bias, out_weight, out_bias)])
    per = 2 if blocks[FINE] % 2 == 0 else 1
    return pl.pallas_call(
        lift_kernel,
        grid=(blocks[FINE] // per,),
        out_shape=jax.ShapeDtypeStruct((2 * blocks[FINE], wide, channels), jnp.bfloat16),
        in_specs=[vmem, vmem],
        out_specs=pl.BlockSpec((2 * per, wide, channels), lambda g: (g, 0, 0)),
        compiler_params=pltpu.CompilerParams(vmem_limit_bytes=8 * 1024 * 1024),
    )(lines, table)


def solution(mesh):
    rows = P(("img", "rows"), None, None)
    return jax.shard_map(
        functools.partial(local, mesh.shape["rows"]),
        mesh=mesh,
        in_specs=(rows, rows, rows, P(), P(), P(), P()),
        out_specs=rows,
        check_vma=False,
    )
```

time: 35.8 us -> 33.1 us (0.925)
  Pallas kernels: 35.4 us -> 32.9 us
    pallas_call x1, Pallas kernels: 32.9 us -> 30.4 us  [local(): pl.pallas_call(functools.partial(kernel, devices), out_shape=[jax.ShapeDt...]
where the time goes in v2:
time: 33.1 us; the launch traced here: 32.9 us
  Pallas kernels  32.9 us (99%)
    pallas_call x1, Pallas kernels, local(): pl.pallas_call(functools.partial(kernel, devices), out_shape=[jax.ShapeDt...  30.4 us
    pallas_call x1, Pallas kernels, local(): pl.pallas_call(lift_kernel, grid=(blocks[FINE] // per,), out_shape=jax.Sh...  2.53 us

profile of v2, /device:TPU:4, one launch (start us, length us, event | category | flops | bytes accessed | tf_op | source)
XLA Modules:
  0.0 32.9 jit_solution(8255929169754594349)
XLA Ops:
  0.0 30.4 %shard_map.73 = (bf16[10,8,16,256]{3,2,1,0:T(8,128)(2,1)S(1)}, bf16[512,256]{1,0:T(8,128)(2,1)S(1)}) custom-call(bf16[8,128,256]{2,1,0:T(8,128)(2,1)} %fine_hbm.1, bf16[4,64,256]{2,1,0:T(8,128)(2,1)} %second_hbm.1, bf16[2,32,256]{2,1,0:T(8,128)(2,1)} %third_hbm.1, bf16[10,2304,256]{2,1,0:T(8,128)(2,1)} %bitcast.1, f32[10,256]{1,0:T(8,128)} %bias_hbm.1, ...), custom_call_target="tpu_custom_call" | custom-call | tf_op jit(solution)/shard_map/pallas_call | solution.py:523
  30.4 2.5 %shard_map.74 = bf16[16,256,256]{2,1,0:T(8,128)(2,1)} custom-call(bf16[10,8,16,256]{3,2,1,0:T(8,128)(2,1)S(1)} %get-tuple-element.7.lines_ref, bf16[512,256]{1,0:T(8,128)(2,1)S(1)} %get-tuple-element.8.table_ref), custom_call_target="tpu_custom_call" | custom-call | tf_op jit(solution)/shard_map/pallas_call | solution.py:535

commit v3 on v2

--- a/solution.py
+++ b/solution.py
@@ -9,9 +9,9 @@
 
 MESH = pl.DeviceIdType.MESH
 LANES = 16
-VMEM_MIB = 44
+VMEM_MIB = 52
 MOST = 640
-RING = 2
+RING = 1
 FINE, SECOND, THIRD = 0, 1, 2
 HALOS = (5, 6, 5)
 WEIGHT_ORDER = (6, 7, 2, 0, 1, 3, 4, 5, 8, 9)
@@ -30,14 +30,14 @@
         cuts = [block, block // 2, 0] if block > 1 else [block, 0]
         return [(low, high - low, True) for high, low in zip(cuts, cuts[1:])]
     away, beside = list(range(block - 1, -1, -1)), list(range(block))
-    order = away[:RING] + beside[:RING] + away[RING:near]
+    order = away[:2] + beside[:RING] + away[2:near]
     order = list(dict.fromkeys(order + beside[:near] + away))
     return [(r, 1, r >= block - near) for r in order]
 
 
-def pairs_of(first, last, most):
+def parts_of(first, last, most):
     rows = last - first
-    parts = min(rows, 2 * -(-rows // (2 * most)))
+    parts = -(-rows // most)
     cuts = [first + rows * i // parts for i in range(parts + 1)]
     return [(p, q - p) for p, q in zip(cuts, cuts[1:])]
 
@@ -57,7 +57,7 @@
     fine_ref, second_ref, third_ref, bias_ref, proj_bias_ref,
     fine_other, second_other, third_other,
     second_up, second_down, third_up, third_down,
-    fine_x, second_x, third_x, stage, weights, projs,
+    fine_x, second_x, third_x, stage, weights, mixed, projs,
     padded_f, hidden_f, addend_f, joined_f, hidden2_f, merged_f, path_f,
     padded_s, hidden_s, merged_s, path_s,
     padded_t, hidden_t, refined_f, refined_s, refined_t, proj_y,
@@ -205,22 +205,40 @@
             if valid is not None:
                 row = jnp.where(valid, row, 0.0)
             before, after = edge_steps(row, False)
-            ref[at + r, 1:steps + 1] = row[0].astype(jnp.bfloat16)
-            ref[at + r, 0] = before[0].astype(jnp.bfloat16)
-            ref[at + r, steps + 1] = after[0].astype(jnp.bfloat16)
+            line = [before[0]] + [row[0, t] for t in range(steps)] + [after[0]]
+            for pair in range(steps // 2):
+                d0, d1, d2, d3 = line[2 * pair:2 * pair + 4]
+                for kind, value in enumerate((d0 - d2, d1 + d2, d2 - d1, d1 - d3)):
+                    ref[at + r, kind, pair] = value.astype(jnp.bfloat16)
+
+    def mix_taps(k):
+        weight_copies[k].wait()
+        for a in range(3):
+            sides = 0.5 * (weights[k, a, 0].astype(jnp.float32) + weights[k, a, 2].astype(jnp.float32))
+            middle = 0.5 * weights[k, a, 1].astype(jnp.float32)
+            mixed[k, 0, a] = (sides + middle).astype(jnp.bfloat16)
+            mixed[k, 1, a] = (sides - middle).astype(jnp.bfloat16)
 
     def conv(ref, k, tiles, emit):
-        steps = ref.shape[1] - 2
+        half, channels = ref.shape[2], ref.shape[4]
+        bias = bias_ref[k:k + 1, :]
+        taps = [[weights[k, a, 0] for a in range(3)], [mixed[k, 0, a] for a in range(3)],
+                [mixed[k, 1, a] for a in range(3)], [weights[k, a, 2] for a in range(3)]]
         for r, rows in tiles:
-            flat = jnp.concatenate(
-                [ref[r + a:r + a + rows, b:b + steps].reshape(rows * steps * LANES, -1)
-                 for a in range(3) for b in range(3)], axis=1)
-            acc = jnp.dot(flat, weights[k], preferred_element_type=jnp.float32)
-            acc = acc + bias_ref[k:k + 1, :]
-            emit(r, acc.reshape(rows, steps, LANES, -1))
+            parts = []
+            for kind in range(4):
+                flat = jnp.concatenate(
+                    [ref[r + a:r + a + rows, kind].reshape(rows * half * LANES, channels) for a in range(3)], axis=1)
+                parts.append(jnp.dot(
+                    flat, jnp.concatenate(taps[kind], axis=0), preferred_element_type=jnp.float32))
+            left = bias + parts[0] + parts[1] + parts[2]
+            right = bias + parts[1] - parts[2] - parts[3]
+            shape = (rows, half, 1, LANES, channels)
+            acc = jnp.concatenate([left.reshape(shape), right.reshape(shape)], axis=2)
+            emit(r, acc.reshape(rows, 2 * half, LANES, channels))
 
     def tiles_of(level, first, last):
-        return pairs_of(first, last, max(1, MOST // own[level].shape[1]))
+        return parts_of(first, last, max(1, MOST // own[level].shape[1]))
 
     def raw_row(level, place):
         block, halo = blocks[level], HALOS[level]
@@ -339,31 +357,34 @@
             lines_f[r:r + rows] = y.astype(jnp.bfloat16).reshape(rows, refined_f.shape[1], LANES, -1)
 
     take_rows(FINE, padded_f, 0, block_f)
-    weight_copies[6].wait()
+    mix_taps(6)
+    mix_taps(7)
     hidden(FINE, padded_f, hidden_f, 6, tiles_of(FINE, halo_f, halo_f + block_f - 2), 1 - halo_f)
-    weight_copies[7].wait()
     fine_unit(tiles_of(FINE, halo_f, halo_f + block_f - 4))
-    for at in range(len(pair_copies[SECOND])):
-        pass_on(SECOND, at)
+    pass_on(SECOND, 0)
+    mix_taps(2)
     take_rows(THIRD, padded_t, 0, block_t)
     take_rows(SECOND, padded_s, 0, block_s)
+    for at in range(1, len(pair_copies[SECOND])):
+        pass_on(SECOND, at)
+    mix_taps(0)
+    mix_taps(1)
+    mix_taps(3)
     fill_table(table, own[FINE].shape[1])
     pass_on(THIRD, 0)
+    for k in (4, 5, 8, 9):
+        mix_taps(k)
 
     last_s = block_s + 2 * halo_s
     arrive(SECOND)
     pass_on(FINE, 0)
     take_rows(SECOND, padded_s, -halo_s, 0)
     take_rows(SECOND, padded_s, block_s, block_s + halo_s)
-    weight_copies[2].wait()
     hidden(SECOND, padded_s, hidden_s, 2, tiles_of(SECOND, 0, last_s - 2), 1 - halo_s)
     arrive(THIRD)
     pass_on(FINE, 1)
     take_rows(THIRD, padded_t, -halo_t, 0)
     take_rows(THIRD, padded_t, block_t, block_t + halo_t)
-    weight_copies[0].wait()
-    weight_copies[1].wait()
-    weight_copies[3].wait()
     proj_copy.wait()
     hidden(THIRD, padded_t, hidden_t, 0, tiles_of(THIRD, 0, block_t + 2 * halo_t - 2), 1 - halo_t)
 
@@ -386,8 +407,6 @@
     pass_on(FINE, 2)
     pass_on(FINE, 3)
 
-    weight_copies[4].wait()
-    weight_copies[5].wait()
     hidden(SECOND, padded_s, hidden_s, 4, tiles_of(SECOND, 0, last_s - 6), 3 - halo_s)
 
     def emit_refined(r, acc):
@@ -408,17 +427,14 @@
     take_rows(FINE, padded_f, block_f, block_f + ring)
     hidden(FINE, padded_f, hidden_f, 6, [(halo_f - ring, ring), (halo_f + block_f - 2, ring)], 1 - halo_f)
     fine_unit([(halo_f - ring, ring), (halo_f + block_f - 4, ring)])
-    low, high = halo_f - 2, halo_f - 2 + block_f
+    low, high = halo_f - ring, halo_f + block_f - 4 + ring
+    pass_on(FINE, 5)
     fine_join(low, high)
-    pass_on(FINE, 5)
-    weight_copies[8].wait()
-    weight_copies[9].wait()
     hidden(FINE, joined_f, hidden2_f, 8, tiles_of(FINE, low, high - 2), 3 - halo_f)
-    pass_on(FINE, 6)
     fine_refined(tiles_of(FINE, low, high - 4))
     project(tiles_of(FINE, low, high - 4))
 
-    for at in range(7, len(order)):
+    for at in range(6, len(order)):
         pass_on(FINE, at)
     for at, row in enumerate(order):
         if far_copies[FINE][at] is not None and row < block_f - ring:
@@ -491,8 +507,11 @@
     def raw(count, level):
         return pltpu.VMEM((count, columns[level], channels), jnp.bfloat16)
 
-    def rows_of(count, level, extra=0, dtype=jnp.bfloat16):
-        return pltpu.VMEM((count, steps[level] + extra, LANES, channels), dtype)
+    def rows_of(count, level, dtype=jnp.bfloat16):
+        return pltpu.VMEM((count, steps[level], LANES, channels), dtype)
+
+    def mixed_rows(count, level):
+        return pltpu.VMEM((count, 4, steps[level] // 2, LANES, channels), jnp.bfloat16)
 
     extents = [block + 2 * halo for block, halo in zip(blocks, HALOS)]
     copies = sum(len(direct_rows(level, blocks[level])) for level in (SECOND, THIRD))
@@ -505,17 +524,19 @@
     scratch += [raw(HALOS[level], level) for level in (SECOND, THIRD) for _ in range(2)]
     scratch += [rows_of(extents[level], level) for level in range(3)]
     scratch += [pltpu.VMEM((8, channels // width, columns[FINE], width), jnp.float32)]
-    scratch += [pltpu.VMEM((conv_weight.shape[0], 9 * channels, channels), jnp.bfloat16),
+    convs = conv_weight.shape[0]
+    scratch += [pltpu.VMEM((convs, 3, 3, channels, channels), jnp.bfloat16),
+                pltpu.VMEM((convs, 2, 3, channels, channels), jnp.bfloat16),
                 pltpu.VMEM(out_weight.shape, jnp.bfloat16)]
-    scratch += [rows_of(extents[FINE], FINE, 2), rows_of(extents[FINE] - 2, FINE, 2),
-                rows_of(extents[FINE] - 4, FINE, 0, jnp.float32), rows_of(extents[FINE] - 4, FINE, 2),
-                rows_of(extents[FINE] - 6, FINE, 2), rows_of(extents[FINE] - 4, FINE), rows_of(extents[FINE] - 4, FINE)]
-    scratch += [rows_of(extents[SECOND], SECOND, 2), rows_of(extents[SECOND] - 2, SECOND, 2),
+    scratch += [mixed_rows(extents[FINE], FINE), mixed_rows(extents[FINE] - 2, FINE),
+                rows_of(extents[FINE] - 4, FINE, jnp.float32), mixed_rows(extents[FINE] - 4, FINE),
+                mixed_rows(extents[FINE] - 6, FINE), rows_of(extents[FINE] - 4, FINE), rows_of(extents[FINE] - 4, FINE)]
+    scratch += [mixed_rows(extents[SECOND], SECOND), mixed_rows(extents[SECOND] - 2, SECOND),
                 rows_of(extents[SECOND] - 4, SECOND), rows_of(extents[SECOND] - 4, SECOND)]
-    scratch += [rows_of(extents[THIRD], THIRD, 2), rows_of(extents[THIRD] - 2, THIRD, 2)]
+    scratch += [mixed_rows(extents[THIRD], THIRD), mixed_rows(extents[THIRD] - 2, THIRD)]
     scratch += [rows_of(extents[FINE] - 8, FINE), rows_of(extents[SECOND] - 8, SECOND),
                 rows_of(extents[THIRD] - 4, THIRD)]
-    scratch += [rows_of(max(extents[SECOND] - 8, extents[THIRD] - 4), SECOND, 0, jnp.float32)]
+    scratch += [rows_of(max(extents[SECOND] - 8, extents[THIRD] - 4), SECOND, jnp.float32)]
     scratch += [dma((copies,)) for _ in range(6)] + [dma((pairs,)) for _ in range(4)]
     scratch += [dma((conv_weight.shape[0],)), dma, dma((5,))]
     vmem, far = pl.BlockSpec(memory_space=pltpu.VMEM), pl.BlockSpec(memory_space=pltpu.HBM)
@@ -530,7 +551,7 @@
         compiler_params=pltpu.CompilerParams(
             collective_id=0, has_side_effects=True, vmem_limit_bytes=VMEM_MIB * 1024 * 1024),
     )(*[pltpu.with_memory_space_constraint(v, pltpu.HBM) for v in (
-        *fields, conv_weight.reshape(conv_weight.shape[0], 9 * channels, channels), conv_bias, out_weight, out_bias)])
+        *fields, conv_weight.reshape(convs, 3, 3, channels, channels), conv_bias, out_weight, out_bias)])
     per = 2 if blocks[FINE] % 2 == 0 else 1
     return pl.pallas_call(
         lift_kernel,

time: 33.1 us -> 30.4 us (0.918)
  Pallas kernels: 32.9 us -> 30.3 us
    pallas_call x1, Pallas kernels: 30.4 us -> 27.7 us  [local(): pl.pallas_call(functools.partial(kernel, devices), out_shape=[jax.ShapeDt...]
where the time goes in v3:
time: 30.4 us; the launch traced here: 30.3 us
  Pallas kernels  30.3 us (100%)
    pallas_call x1, Pallas kernels, local(): pl.pallas_call(functools.partial(kernel, devices), out_shape=[jax.ShapeDt...  27.7 us
    pallas_call x1, Pallas kernels, local(): pl.pallas_call(lift_kernel, grid=(blocks[FINE] // per,), out_shape=jax.Sh...  2.53 us

profile of v3, /device:TPU:4, one launch (start us, length us, event | category | flops | bytes accessed | tf_op | source)
XLA Modules:
  0.0 30.3 jit_solution(12838540351186492894)
XLA Ops:
  0.0 27.7 %shard_map.73 = (bf16[10,8,16,256]{3,2,1,0:T(8,128)(2,1)S(1)}, bf16[512,256]{1,0:T(8,128)(2,1)S(1)}) custom-call(bf16[8,128,256]{2,1,0:T(8,128)(2,1)} %fine_hbm.1, bf16[4,64,256]{2,1,0:T(8,128)(2,1)} %second_hbm.1, bf16[2,32,256]{2,1,0:T(8,128)(2,1)} %third_hbm.1, bf16[10,3,3,256,256]{4,3,2,1,0:T(8,128)(2,1)} %bitcast.1, f32[10,256]{1,0:T(8,128)} %bias_hbm.1, ...), custom_call_target="tpu_custom_call" | custom-call | tf_op jit(solution)/shard_map/pallas_call | solution.py:544
  27.7 2.5 %shard_map.74 = bf16[16,256,256]{2,1,0:T(8,128)(2,1)} custom-call(bf16[10,8,16,256]{3,2,1,0:T(8,128)(2,1)S(1)} %get-tuple-element.7.lines_ref, bf16[512,256]{1,0:T(8,128)(2,1)S(1)} %get-tuple-element.8.table_ref), custom_call_target="tpu_custom_call" | custom-call | tf_op jit(solution)/shard_map/pallas_call | solution.py:556

commit v4 on v3

--- a/solution.py
+++ b/solution.py
@@ -480,20 +480,28 @@
             table[half * wide:(half + 1) * wide, side * columns:(side + 1) * columns] = weight.astype(jnp.bfloat16)
 
 
-def lift_kernel(lines_ref, table_ref, out_ref):
-    at = pl.program_id(0)
-    steps, channels = lines_ref.shape[1], lines_ref.shape[3]
+def lift_kernel(lines_ref, table_ref, out_hbm, rows_ref, sems):
+    count, steps, channels = lines_ref.shape[0], lines_ref.shape[1], lines_ref.shape[3]
     columns = steps * LANES
     wide = 2 * columns
-    per = out_ref.shape[0] // 2
-    for i in range(per + 1):
-        pair = lines_ref[pl.ds(at * per + i, 2)].reshape(2 * columns, channels)
-        first, last = (wide if i == 0 else 0), (wide if i == per else 2 * wide)
+    pairs = count - 1
+    sent, copies = 0, []
+    for i in range(pairs):
+        pair = lines_ref[i:i + 2].reshape(2 * columns, channels)
+        first, last = (wide if i == 0 else 0), (wide if i == pairs - 1 else 2 * wide)
         rows = jnp.dot(table_ref[first:last], pair, preferred_element_type=jnp.float32).astype(jnp.bfloat16)
         if i > 0:
-            out_ref[2 * i - 1] = rows[0:wide]
-        if i < per:
-            out_ref[2 * i] = rows[last - first - wide:]
+            rows_ref[2 * i - 1] = rows[0:wide]
+        if i < pairs - 1:
+            rows_ref[2 * i] = rows[last - first - wide:]
+        ready = min(2 * i + 1, 2 * pairs - 2)
+        if i in (2 * pairs // 3, pairs - 1) and ready > sent:
+            part = pl.ds(sent, ready - sent)
+            copies.append(pltpu.make_async_copy(rows_ref.at[part], out_hbm.at[part], sems.at[len(copies)]))
+            copies[-1].start()
+            sent = ready
+    for copy in copies:
+        copy.wait()
 
 
 def local(devices, feat_fine, feat_second, feat_third, conv_weight, conv_bias, out_weight, out_bias):
@@ -552,13 +560,13 @@
             collective_id=0, has_side_effects=True, vmem_limit_bytes=VMEM_MIB * 1024 * 1024),
     )(*[pltpu.with_memory_space_constraint(v, pltpu.HBM) for v in (
         *fields, conv_weight.reshape(convs, 3, 3, channels, channels), conv_bias, out_weight, out_bias)])
-    per = 2 if blocks[FINE] % 2 == 0 else 1
+    shape = (2 * blocks[FINE], wide, channels)
     return pl.pallas_call(
         lift_kernel,
-        grid=(blocks[FINE] // per,),
-        out_shape=jax.ShapeDtypeStruct((2 * blocks[FINE], wide, channels), jnp.bfloat16),
+        out_shape=jax.ShapeDtypeStruct(shape, jnp.bfloat16),
         in_specs=[vmem, vmem],
-        out_specs=pl.BlockSpec((2 * per, wide, channels), lambda g: (g, 0, 0)),
+        out_specs=far,
+        scratch_shapes=[pltpu.VMEM(shape, jnp.bfloat16), dma((2,))],
         compiler_params=pltpu.CompilerParams(vmem_limit_bytes=8 * 1024 * 1024),
     )(lines, table)
 

time: 30.4 us -> 30 us (0.987)
  Pallas kernels: 30.3 us -> 29.7 us
    pallas_call x1, Pallas kernels: 2.53 us -> 1.97 us  [local(): pl.pallas_call(lift_kernel, out_shape=jax.ShapeDtypeStruct(shape, jnp.bfl...]
where the time goes in v4:
time: 30 us; the launch traced here: 29.9 us
  Pallas kernels  29.7 us (99%)
    pallas_call x1, Pallas kernels, local(): pl.pallas_call(functools.partial(kernel, devices), out_shape=[jax.ShapeDt...  27.7 us
    pallas_call x1, Pallas kernels, local(): pl.pallas_call(lift_kernel, out_shape=jax.ShapeDtypeStruct(shape, jnp.bfl...  1.97 us

profile of v4, /device:TPU:4, one launch (start us, length us, event | category | flops | bytes accessed | tf_op | source)
XLA Modules:
  0.0 29.9 jit_solution(4708416430943026882)
XLA Ops:
  0.0 27.7 %shard_map.73 = (bf16[10,8,16,256]{3,2,1,0:T(8,128)(2,1)S(1)}, bf16[512,256]{1,0:T(8,128)(2,1)S(1)}) custom-call(bf16[8,128,256]{2,1,0:T(8,128)(2,1)} %fine_hbm.1, bf16[4,64,256]{2,1,0:T(8,128)(2,1)} %second_hbm.1, bf16[2,32,256]{2,1,0:T(8,128)(2,1)} %third_hbm.1, bf16[10,3,3,256,256]{4,3,2,1,0:T(8,128)(2,1)} %bitcast.1, f32[10,256]{1,0:T(8,128)} %bias_hbm.1, ...), custom_call_target="tpu_custom_call" | custom-call | tf_op jit(solution)/shard_map/pallas_call | solution.py:552
  27.7 2.0 %shard_map.74 = bf16[16,256,256]{2,1,0:T(8,128)(2,1)} custom-call(bf16[10,8,16,256]{3,2,1,0:T(8,128)(2,1)S(1)} %get-tuple-element.7.lines_ref, bf16[512,256]{1,0:T(8,128)(2,1)S(1)} %get-tuple-element.8.table_ref), custom_call_target="tpu_custom_call" | custom-call | tf_op jit(solution)/shard_map/pallas_call | solution.py:564
